TPU v7x, 32 devices: a whole 2x2x4 slice. The times are simulated.
32 devices in a mesh: img: 8 (over y, x, core), ori: 4 (over z).
Axes of the slice: x: 2, y: 2, z: 4, core: 2. Of those that a mesh axis runs over, the one named last changes fastest.
Arguments:
- images: bfloat16 [4096, 4096], P('img'), may hold values from -6 to 6
- ctf_class: int32 [4096], P('img'), may hold values from 0 to 15
- class_mask: int32 [4096, 8], P('img'), may hold values from 0 to 1, as said below
- precision: float32 [4096], P('img'), may hold values from 0.02 to 0.5
- class_log_prior: float32 [4096, 8], P('img'), may hold values from -6 to 406
- ctf_filters: float32 [16, 4096], replicated, may hold values from -1 to 1
- volume_coef: bfloat16 [8, 16, 2, 4096], P(None, 'img'), may hold values from -6 to 6
- slice_ops: bfloat16 [8, 4096, 64], replicated, may hold values from -0.09375 to 0.09375
- tilt_index: int32 [64], P('ori'), may hold values from 0 to 7
- azimuth_index: int32 [64], P('ori'), may hold values from 0 to 31
Outputs:
- coef_sum: float32 [8, 16, 2, 4096], P(None, 'img')
- log_evidence: float32 [4096], P('img')
- class_posterior: float32 [4096, 8], P('img')
Inputs may be any that keep to these rules, and one draw needn't show every extreme that they name: `class_mask`: every image allows at least one class.
All inputs are finite; a program needn't handle non-finite values.
Results may differ from a plain program's by a relative error of at most 0.024.
The roundings to bfloat16 on the way count: a program that leaves them out, or rounds other values in their place, can miss the bound.
Values may be sent and summed in bfloat16 or wider, within the bound.
No kernel may reach another device: no remote copies, remote signals or barrier semaphores. Data moves between devices by JAX's collectives and lax.ppermute only.
A program may use at most 192 MiB of HBM per device.

v0:
```python
import math
import jax
import jax.numpy as jnp
from jax import lax
from jax.sharding import PartitionSpec as P

ORD = 64
ANG = 128
NAZI = 32
LM = 4096


def synth_table():
    orders = (jnp.arange(ORD) - ORD // 2).astype(jnp.float32)
    angles = jnp.arange(ANG).astype(jnp.float32) * (2.0 * math.pi / ANG)
    phase = orders[:, None] * angles[None, :]
    cosine = jnp.cos(phase)
    sine = jnp.sin(phase)
    upper = jnp.concatenate([cosine, sine], axis=1)
    lower = jnp.concatenate([-sine, cosine], axis=1)
    return (jnp.concatenate([upper, lower], axis=0) * ORD ** (-0.5)).astype(jnp.bfloat16)


def rotated_ops(tilts, azimuths, slice_ops):
    chosen = jnp.take(slice_ops, tilts, axis=0).astype(jnp.float32)
    chosen = jnp.transpose(chosen, (1, 0, 2))
    orders = (jnp.arange(LM) % ORD - ORD // 2).astype(jnp.float32)
    turns = azimuths.astype(jnp.float32) * (2.0 * math.pi / NAZI)
    phase = orders[:, None] * turns[None, :]
    cosine = jnp.cos(phase)[:, :, None]
    sine = jnp.sin(phase)[:, :, None]
    upper = jnp.concatenate([cosine * chosen, -sine * chosen], axis=2)
    lower = jnp.concatenate([sine * chosen, cosine * chosen], axis=2)
    rotator = jnp.concatenate([upper, lower], axis=0)
    return rotator.reshape(2 * LM, -1).astype(jnp.bfloat16)


def synthesize(coefs, rotator, angle_table):
    classes, radial = (coefs.shape[0], coefs.shape[1])
    flat_coef = coefs.reshape(classes * radial, 2 * LM)
    harmonics = jnp.dot(flat_coef, rotator, preferred_element_type=jnp.float32).astype(jnp.bfloat16)
    orients = rotator.shape[1] // (2 * ORD)
    harmonics = (
        harmonics.reshape(classes, radial, orients, 2 * ORD)
        .transpose(2, 0, 1, 3)
        .reshape(-1, 2 * ORD)
    )
    values = jnp.dot(harmonics, angle_table, preferred_element_type=jnp.float32).astype(
        jnp.bfloat16
    )
    return values.reshape(orients * classes, radial * 2 * ANG)


def adjoint(back_proj, rotator, angle_table, radial, classes):
    columns = back_proj.shape[1]
    orients = rotator.shape[1] // (2 * ORD)
    spread = (
        back_proj.reshape(radial, 2 * ANG, columns)
        .transpose(0, 2, 1)
        .reshape(radial * columns, 2 * ANG)
    )
    harmonics = jnp.dot(spread, angle_table.T, preferred_element_type=jnp.float32).astype(
        jnp.bfloat16
    )
    harmonics = harmonics.reshape(radial, orients, classes, 2 * ORD).transpose(2, 0, 1, 3)
    harmonics = harmonics.reshape(classes * radial, orients * 2 * ORD)
    return lax.dot_general(
        harmonics, rotator, (((1,), (1,)), ((), ())), preferred_element_type=jnp.float32
    )


def body(
    images,
    ctf_class,
    class_mask,
    precision,
    class_log_prior,
    ctf_filters,
    volume_coef,
    slice_ops,
    tilt_index,
    azimuth_index,
):
    angle_table = synth_table()
    image_rows = images.shape[0]
    classes = volume_coef.shape[0]
    radial = volume_coef.shape[1]
    orients = tilt_index.shape[0]
    filter_count = ctf_filters.shape[0]
    selector = (ctf_class[:, None] == jnp.arange(filter_count)[None, :]).astype(jnp.float32)
    ctf_rows = jnp.dot(selector, ctf_filters, precision=lax.Precision.HIGHEST)
    filtered = (images.astype(jnp.float32) * ctf_rows).astype(jnp.bfloat16)
    ctf_square = ctf_filters * ctf_filters
    rotator = rotated_ops(tilt_index, azimuth_index, slice_ops)
    coefs = lax.all_gather(volume_coef, "img", axis=1, tiled=True)
    templates = synthesize(coefs, rotator, angle_table)
    part_img = filtered
    correl = lax.dot_general(
        part_img, templates, (((1,), (1,)), ((), ())), preferred_element_type=jnp.float32
    )
    square = templates.astype(jnp.float32)
    square = square * square
    energy = lax.dot_general(
        ctf_square, square, (((1,), (1,)), ((), ())), precision=lax.Precision.HIGHEST
    )
    correl, energy = (correl, energy)
    energy_rows = jnp.dot(selector, energy, precision=lax.Precision.HIGHEST)
    score = precision[:, None] * (correl - 0.5 * energy_rows) + jnp.tile(
        class_log_prior, (1, orients)
    )
    allowed = jnp.tile(class_mask, (1, orients)) > 0
    score = jnp.where(allowed, score, -1e30)
    row_peak = lax.pmax(jnp.max(score, axis=1), "ori")
    exponent = jnp.exp(score - row_peak[:, None])
    local_totals = exponent.reshape(image_rows, orients, classes).sum(axis=1)
    totals = lax.psum(local_totals, "ori")
    norm_sum = totals.sum(axis=1)
    log_evidence = row_peak + jnp.log(norm_sum)
    class_posterior = totals / norm_sum[:, None]
    weights = (exponent / norm_sum[:, None]).astype(jnp.bfloat16)
    part_img = filtered
    summed = lax.psum_scatter(
        lax.dot_general(
            part_img, weights, (((0,), (0,)), ((), ())), preferred_element_type=jnp.float32
        ).astype(jnp.bfloat16),
        "img",
        scatter_dimension=0,
        tiled=True,
    )
    coef_own = adjoint(summed, rotator, angle_table, radial, classes)
    coef_sum = (
        lax.psum(coef_own.astype(jnp.bfloat16), "ori")
        .astype(jnp.float32)
        .reshape(classes, radial, 2, LM)
    )
    return (coef_sum, log_evidence, class_posterior)


def solution(mesh):
    placed = (
        P("img", None),
        P("img"),
        P("img", None),
        P("img"),
        P("img", None),
        P(),
        P(None, "img", None, None),
        P(),
        P("ori"),
        P("ori"),
    )
    return jax.shard_map(
        body,
        mesh=mesh,
        in_specs=placed,
        out_specs=(P(None, "img", None, None), P("img"), P("img", None)),
        check_vma=False,
    )
```

profile of v0, /device:TPU:0, one launch (start us, length us, event | category | flops | bytes accessed | tf_op | source)
XLA Modules:
  0.0 214.8 jit_solution(3780529455137462611)
XLA Ops:
  7.2 0.7 all-gather.2.cloned.1.call-update
  8.0 0.7 compare_select_fusion
  8.6 0.7 compare_and_fusion
  9.3 0.7 convert_multiply_fusion.1
  9.9 0.7 broadcast_compare_fusion
  10.7 1.0 fusion.21
  11.9 7.0 %gather_fusion = bf16[16,4096,64]{1,2,0:T(8,128)(2,1)} fusion(bf16[8,4096,64]{1,2,0:T(8,128)(2,1)} %param.17, s32[1024]{0:T(1024)S(1)} %pad_clamp_fusion), kind=kCustom, calls=%fused_computation | custom fusion | bytes 16777280 | tf_op jit(solution)/shard_map/jit(_take)/gather | solution.py:25
  18.9 6.9 %multiply_convert_fusion = bf16[512,4096]{1,0:T(8,128)(2,1)} fusion(bf16[512,4096]{1,0:T(8,128)(2,1)} %param.10, f32[16,4096]{1,0:T(8,128)S(1)} %copy-done, s32[512]{0:T(512)S(1)} %copy-done.2), kind=kOutput, calls=%fused_computation.13 | convolution fusion | flops 408952832 | bytes 8652800 | tf_op jit(solution)/shard_map/dot_general | solution.py:91
  25.9 11.8 %fusion.3 = (bf16[4096,16,64]{0,2,1:T(8,128)(2,1)}, bf16[4096,16,64]{0,2,1:T(8,128)(2,1)}, bf16[4096,16,64]{0,2,1:T(8,128)(2,1)}) fusion(f32[4096,16]{0,1:T(8,128)S(1)} %get-tuple-element.8, bf16[16,4096,64]{1,2,0:T(8,128)(2,1)} %gather_fusion, pred[16]{0:T(512)(128)(4,1)S(1)} %compare_and_fusion, f32[4096,16]{0,1:T(8,128)S(1)} %get-tuple-element.9, ...), kind=kLoop, calls=%fused_computation.10 | loop fusion | flops 33554432 | bytes 34340880 | tf_op jit(solution)/shard_map/convert.9
  37.6 25.2 %pad_maximum_fusion.3 = (bf16[4096,16,128]{0,2,1:T(8,128)(2,1)}, bf16[4096,16,128]{0,2,1:T(8,128)(2,1)}) fusion(bf16[4096,16,64]{0,2,1:T(8,128)(2,1)} %get-tuple-element.3, bf16[4096,16,64]{0,2,1:T(8,128)(2,1)} %get-tuple-element.5, bf16[4096,16,64]{0,2,1:T(8,128)(2,1)} %get-tuple-element.4), kind=kLoop, calls=%fused_computation.4 | loop fusion | flops 67108864 | bytes 58720256 | tf_op jit(solution)/shard_map/concatenate | solution.py:32
  62.9 2.9 %copy.17 = bf16[16,8,2,4096]{3,1,2,0:T(8,128)(2,1)S(1)} copy(bf16[16,8,2,4096]{3,2,1,0:T(2,128)(2,1)} %bitcast.55) | data formatting | bytes 4194304
  65.8 14.6 %fusion.7 = bf16[128,2048]{0,1:T(8,128)(2,1)S(1)} fusion(bf16[128,8192]{1,0:T(8,128)(2,1)S(1)} %bitcast.56, bf16[4096,2048]{0,1:T(8,128)(2,1)} %bitcast.52, bf16[4096,2048]{0,1:T(8,128)(2,1)} %bitcast.50), kind=kOutput, calls=%fused_computation.18 | convolution fusion | flops 4362338304 | bytes 36175872 | tf_op jit(solution)/shard_map/dot_general | solution.py:41
  81.3 0.7 reshape.165
  82.0 1.7 fusion.8
  83.8 3.7 %fusion.35 = f32[512,128]{0,1:T(8,128)S(1)} fusion(bf16[512,4096]{1,0:T(8,128)(2,1)} %multiply_convert_fusion, bf16[128,4096]{1,0:T(8,128)(2,1)S(1)} %reshape.165), kind=kOutput, calls=%fused_computation.67 | convolution fusion | flops 536870912 | bytes 5505024 | tf_op jit(solution)/shard_map/dot_general | solution.py:98
  88.0 13.5 %pmax.7 = f32[512]{0:T(512)S(1)} all-reduce(f32[512]{0:T(512)S(1)} %get-tuple-element.14), channel_id=1, replica_groups=mesh['img'=8,'ori'=4] {'ori'}, use_global_device_ids=true, to_apply=%region_1.2 | all-reduce | flops 512 | bytes 4096 | tf_op jit(solution)/shard_map/pmax | solution.py:113
  101.5 15.5 %psum.14 = f32[512,8]{0,1:T(8,128)S(1)} all-reduce(f32[512,8]{0,1:T(8,128)S(1)} %bitcast_reduce_fusion), channel_id=1, replica_groups=mesh['img'=8,'ori'=4] {'ori'}, use_global_device_ids=true, to_apply=%region_3.4 | all-reduce | flops 4096 | bytes 32768 | tf_op jit(solution)/shard_map/psum | solution.py:116
  117.1 4.5 %convolution_convert_fusion = bf16[4096,128]{1,0:T(8,128)(2,1)} fusion(bf16[512,4096]{1,0:T(8,128)(2,1)} %multiply_convert_fusion, f32[512,128]{0,1:T(8,128)S(1)} %get-tuple-element.15, f32[512]{0:T(512)S(1)} %reduce_sum.19, f32[512]{0:T(512)S(1)} %pmax.7), kind=kOutput, calls=%fused_computation.15 | convolution fusion | flops 537591808 | bytes 5509120 | tf_op jit(solution)/shard_map/dot_general | solution.py:123
  121.6 34.6 %reduce-scatter.2.cloned.1.call-done = bf16[512,128]{1,0:T(8,128)(2,1)} async-done(((bf16[4096,128]{1,0:T(8,128)(2,1)}), bf16[512,128]{1,0:T(8,128)(2,1)}) %reduce-scatter.2.cloned.1.call-update) | async-done | bytes 131088 | tf_op jit(solution)/shard_map/reduce_scatter | solution.py:122
  156.3 1.0 copy.15
  157.5 12.1 %fusion.5 = bf16[16,8192]{1,0:T(8,128)(2,1)S(1)} fusion(bf16[4096,2048]{0,1:T(8,128)(2,1)} %bitcast.53, bf16[4096,2048]{0,1:T(8,128)(2,1)} %bitcast.51, bf16[2,8,16,128]{3,2,1,0:T(8,128)(2,1)S(1)} %bitcast.62), kind=kOutput, calls=%fused_computation.12 | convolution fusion | flops 604110848 | bytes 33882112 | tf_op jit(solution)/shard_map/dot_general | solution.py:67
  169.6 0.9 reshape.171
  171.7 34.5 %all-reduce.2.cloned.1.call-done = bf16[8,2,2,4096]{3,2,1,0:T(2,128)(2,1)} async-done(((bf16[8,2,2,4096]{3,2,1,0:T(2,128)(2,1)}), bf16[8,2,2,4096]{3,2,1,0:T(2,128)(2,1)}) %all-reduce.2.cloned.1.call-update) | async-done | bytes 262160 | tf_op jit(solution)/shard_map/psum | solution.py:132
  206.3 2.0 reshape.172
  (31 shorter events, 3.2 us)
Async XLA Ops:
  7.2 55.7 %all-gather.2.cloned.1.call-start = ((), (), s32[]{:S(2)}) async-start(), calls=%async_computation.1 | async-start | bytes 2359296 | tf_op jit(solution)/shard_map/all_gather | solution.py:95
  7.9 148.4 %reduce-scatter.2.cloned.1.call-start = ((), (), s32[]{:S(2)}) async-start(), calls=%async_computation.2 | async-start | bytes 1179648 | tf_op jit(solution)/shard_map/reduce_scatter | solution.py:122
  11.9 7.0 %copy-start = (f32[16,4096]{1,0:T(8,128)S(1)}, f32[16,4096]{1,0:T(8,128)}, u32[]{:S(2)}) copy-start(f32[16,4096]{1,0:T(8,128)} %param.15) | copy-start | bytes 786436
  11.9 7.0 %copy-start.2 = (s32[512]{0:T(512)S(1)}, s32[512]{0:T(512)}, u32[]{:S(2)}) copy-start(s32[512]{0:T(512)} %param.11) | copy-start | bytes 6148
  65.7 21.8 %copy-start.1 = (f32[512,8]{0,1:T(8,128)S(1)}, f32[512,8]{0,1:T(8,128)}, u32[]{:S(2)}) copy-start(f32[512,8]{0,1:T(8,128)} %param.14) | copy-start | bytes 49156
  65.8 21.8 %copy-start.3 = (f32[512]{0:T(512)S(1)}, f32[512]{0:T(512)}, u32[]{:S(2)}) copy-start(f32[512]{0:T(512)} %param.13) | copy-start | bytes 6148
  121.6 84.7 %all-reduce.2.cloned.1.call-start = ((), (), s32[]{:S(2)}) async-start(), calls=%async_computation.3 | async-start | bytes 524288 | tf_op jit(solution)/shard_map/psum | solution.py:132
Sparse Core Ops, SparseCore 0:
  9.9 30.4 all-gather.1
  121.7 34.5 reduce-scatter.1
  170.7 35.5 all-reduce.1
where the time goes:
time: 215 us
  waiting for transfers between devices  69.9 us (33%)
  matrix products  44.7 us (21%)
  other arithmetic  44.1 us (21%)
  blocking collectives  29 us (13%)
  between operations  13.9 us (6%)
  local copies, waits for them, and re-layouts  13 us (6%)
    reduce_scatter x1, waiting for transfers between devices, body(): lax.psum_scatter(lax.dot_general(part_img, weights, (((0,), (0,)), ((), (...  34.6 us
    psum x1, waiting for transfers between devices, body(): lax.psum(coef_own.astype(jnp.bfloat16), 'ori').astype(jnp.float32)  34.5 us
    concatenate x1, other arithmetic, rotated_ops(): upper = jnp.concatenate([cosine * chosen, -sine * chosen], axis=2)  25.2 us
    psum x1, blocking collectives, body(): totals = lax.psum(local_totals, 'ori')  15.5 us
    dot_general x1, matrix products, synthesize(): jnp.dot(flat_coef, rotator, preferred_element_type=jnp.float32)  14.6 us
    pmax x1, blocking collectives, body(): row_peak = lax.pmax(jnp.max(score, axis=1), 'ori')  13.5 us
    dot_general x1, matrix products, adjoint(): lax.dot_general(harmonics, rotator, (((1,), (1,)), ((), ())), preferred_e...  12.1 us
    another operation x1, other arithmetic  11.8 us
  transfers between devices with their start and end apart: 3, of which 2 were waited for; matrix products, arithmetic and copies ran while one was open for 26% of the time, Pallas kernels for 0%

commit v1 on v0

--- a/solution.py
+++ b/solution.py
@@ -129,7 +129,7 @@
     )
     coef_own = adjoint(summed, rotator, angle_table, radial, classes)
     coef_sum = (
-        lax.psum(coef_own.astype(jnp.bfloat16), "ori")
+        jnp.sum(lax.all_gather(coef_own.astype(jnp.bfloat16), "ori"), axis=0)
         .astype(jnp.float32)
         .reshape(classes, radial, 2, LM)
     )

time: 215 us -> 208 us (0.967)
  waiting for transfers between devices: 69.9 us -> 62.3 us
    psum x1 -> x0, waiting for transfers between devices: 34.5 us -> none  [body(): lax.psum(coef_own.astype(jnp.bfloat16), 'ori').astype(jnp.float32)]
    all_gather x0 -> x1, waiting for transfers between devices: none -> 26.9 us  [body(): lax.all_gather(coef_own.astype(jnp.bfloat16), 'ori')]
  transfers between devices with their start and end apart: 3 -> 3, of which waited for: 2 -> 2; matrix products, arithmetic and copies ran while one was open for 26% -> 27% of each run, Pallas kernels for 0% -> 0%
where the time goes in v1:
time: 208 us
  waiting for transfers between devices  62.3 us (30%)
  matrix products  45.3 us (22%)
  other arithmetic  43.6 us (21%)
  blocking collectives  29 us (14%)
  between operations  13.9 us (7%)
  local copies, waits for them, and re-layouts  13.4 us (6%)
    reduce_scatter x1, waiting for transfers between devices, body(): lax.psum_scatter(lax.dot_general(part_img, weights, (((0,), (0,)), ((), (...  34.6 us
    all_gather x1, waiting for transfers between devices, body(): lax.all_gather(coef_own.astype(jnp.bfloat16), 'ori')  26.9 us
    concatenate x1, other arithmetic, rotated_ops(): upper = jnp.concatenate([cosine * chosen, -sine * chosen], axis=2)  25.2 us
    psum x1, blocking collectives, body(): totals = lax.psum(local_totals, 'ori')  15.5 us
    dot_general x1, matrix products, synthesize(): jnp.dot(flat_coef, rotator, preferred_element_type=jnp.float32)  14.6 us
    pmax x1, blocking collectives, body(): row_peak = lax.pmax(jnp.max(score, axis=1), 'ori')  13.5 us
    dot_general x1, matrix products, adjoint(): lax.dot_general(harmonics, rotator, (((1,), (1,)), ((), ())), preferred_e...  12.8 us
    another operation x1, other arithmetic  11.8 us
  transfers between devices with their start and end apart: 3, of which 2 were waited for; matrix products, arithmetic and copies ran while one was open for 27% of the time, Pallas kernels for 0%

profile of v1, /device:TPU:0, one launch (start us, length us, event | category | flops | bytes accessed | tf_op | source)
XLA Modules:
  0.0 207.7 jit_solution(16149064580594544525)
XLA Ops:
  7.2 0.7 all-gather.4.cloned.1.call-update
  8.0 0.7 compare_select_fusion
  8.6 0.7 compare_and_fusion
  9.3 0.7 convert_multiply_fusion.1
  9.9 0.7 broadcast_compare_fusion
  10.7 1.0 fusion.21
  11.9 7.0 %gather_fusion = bf16[16,4096,64]{1,2,0:T(8,128)(2,1)} fusion(bf16[8,4096,64]{1,2,0:T(8,128)(2,1)} %param.17, s32[1024]{0:T(1024)S(1)} %pad_clamp_fusion), kind=kCustom, calls=%fused_computation | custom fusion | bytes 16777280 | tf_op jit(solution)/shard_map/jit(_take)/gather | solution.py:25
  18.9 6.9 %multiply_convert_fusion = bf16[512,4096]{1,0:T(8,128)(2,1)} fusion(bf16[512,4096]{1,0:T(8,128)(2,1)} %param.10, f32[16,4096]{1,0:T(8,128)S(1)} %copy-done, s32[512]{0:T(512)S(1)} %copy-done.2), kind=kOutput, calls=%fused_computation.13 | convolution fusion | flops 408952832 | bytes 8652800 | tf_op jit(solution)/shard_map/dot_general | solution.py:91
  25.9 11.8 %fusion.3 = (bf16[4096,16,64]{0,2,1:T(8,128)(2,1)}, bf16[4096,16,64]{0,2,1:T(8,128)(2,1)}, bf16[4096,16,64]{0,2,1:T(8,128)(2,1)}) fusion(f32[4096,16]{0,1:T(8,128)S(1)} %get-tuple-element.8, bf16[16,4096,64]{1,2,0:T(8,128)(2,1)} %gather_fusion, pred[16]{0:T(512)(128)(4,1)S(1)} %compare_and_fusion, f32[4096,16]{0,1:T(8,128)S(1)} %get-tuple-element.9, ...), kind=kLoop, calls=%fused_computation.10 | loop fusion | flops 33554432 | bytes 34340880 | tf_op jit(solution)/shard_map/convert.10
  37.6 25.2 %pad_maximum_fusion.3 = (bf16[4096,16,128]{0,2,1:T(8,128)(2,1)}, bf16[4096,16,128]{0,2,1:T(8,128)(2,1)}) fusion(bf16[4096,16,64]{0,2,1:T(8,128)(2,1)} %get-tuple-element.3, bf16[4096,16,64]{0,2,1:T(8,128)(2,1)} %get-tuple-element.5, bf16[4096,16,64]{0,2,1:T(8,128)(2,1)} %get-tuple-element.4), kind=kLoop, calls=%fused_computation.4 | loop fusion | flops 67108864 | bytes 58720256 | tf_op jit(solution)/shard_map/concatenate | solution.py:32
  62.9 2.9 %copy.17 = bf16[16,8,2,4096]{3,1,2,0:T(8,128)(2,1)S(1)} copy(bf16[16,8,2,4096]{3,2,1,0:T(2,128)(2,1)} %bitcast.56) | data formatting | bytes 4194304
  65.8 14.6 %fusion.7 = bf16[128,2048]{0,1:T(8,128)(2,1)S(1)} fusion(bf16[128,8192]{1,0:T(8,128)(2,1)S(1)} %bitcast.57, bf16[4096,2048]{0,1:T(8,128)(2,1)} %bitcast.53, bf16[4096,2048]{0,1:T(8,128)(2,1)} %bitcast.51), kind=kOutput, calls=%fused_computation.18 | convolution fusion | flops 4362338304 | bytes 36175872 | tf_op jit(solution)/shard_map/dot_general | solution.py:41
  81.3 0.7 reshape.163
  82.0 1.7 fusion.8
  83.8 3.7 %fusion.35 = f32[512,128]{0,1:T(8,128)S(1)} fusion(bf16[512,4096]{1,0:T(8,128)(2,1)} %multiply_convert_fusion, bf16[128,4096]{1,0:T(8,128)(2,1)S(1)} %reshape.163), kind=kOutput, calls=%fused_computation.67 | convolution fusion | flops 536870912 | bytes 5505024 | tf_op jit(solution)/shard_map/dot_general | solution.py:98
  88.0 13.5 %pmax.7 = f32[512]{0:T(512)S(1)} all-reduce(f32[512]{0:T(512)S(1)} %get-tuple-element.14), channel_id=1, replica_groups=mesh['img'=8,'ori'=4] {'ori'}, use_global_device_ids=true, to_apply=%region_1.2 | all-reduce | flops 512 | bytes 4096 | tf_op jit(solution)/shard_map/pmax | solution.py:113
  101.5 15.5 %psum.7 = f32[512,8]{0,1:T(8,128)S(1)} all-reduce(f32[512,8]{0,1:T(8,128)S(1)} %bitcast_reduce_fusion), channel_id=1, replica_groups=mesh['img'=8,'ori'=4] {'ori'}, use_global_device_ids=true, to_apply=%region_3.4 | all-reduce | flops 4096 | bytes 32768 | tf_op jit(solution)/shard_map/psum | solution.py:116
  117.1 4.5 %convolution_convert_fusion = bf16[4096,128]{1,0:T(8,128)(2,1)} fusion(bf16[512,4096]{1,0:T(8,128)(2,1)} %multiply_convert_fusion, f32[512,128]{0,1:T(8,128)S(1)} %get-tuple-element.15, f32[512]{0:T(512)S(1)} %reduce_sum.31, f32[512]{0:T(512)S(1)} %pmax.7), kind=kOutput, calls=%fused_computation.15 | convolution fusion | flops 537591808 | bytes 5509120 | tf_op jit(solution)/shard_map/dot_general | solution.py:123
  121.6 34.6 %reduce-scatter.2.cloned.1.call-done = bf16[512,128]{1,0:T(8,128)(2,1)} async-done(((bf16[4096,128]{1,0:T(8,128)(2,1)}), bf16[512,128]{1,0:T(8,128)(2,1)}) %reduce-scatter.2.cloned.1.call-update) | async-done | bytes 131088 | tf_op jit(solution)/shard_map/reduce_scatter | solution.py:122
  156.3 1.0 copy.15
  157.5 12.8 %fusion.5 = bf16[16,8192]{1,0:T(8,128)(2,1)} fusion(bf16[4096,2048]{0,1:T(8,128)(2,1)} %bitcast.54, bf16[4096,2048]{0,1:T(8,128)(2,1)} %bitcast.52, bf16[2,8,16,128]{3,2,1,0:T(8,128)(2,1)S(1)} %bitcast.64), kind=kOutput, calls=%fused_computation.12 | convolution fusion | flops 604110848 | bytes 33882112 | tf_op jit(solution)/shard_map/dot_general | solution.py:67
  171.5 26.9 %all-gather.6.cloned.1.call-done = bf16[64,8192]{1,0:T(8,128)(2,1)} async-done(((bf16[16,8192]{1,0:T(8,128)(2,1)}), bf16[64,8192]{1,0:T(8,128)(2,1)}) %all-gather.6.cloned.1.call-update) | async-done | bytes 1048592 | tf_op jit(solution)/shard_map/all_gather | solution.py:132
  198.5 1.5 reduce_sum.32
  199.9 1.3 reshape.169
  (31 shorter events, 3.2 us)
Async XLA Ops:
  7.2 55.7 %all-gather.4.cloned.1.call-start = ((), (), s32[]{:S(2)}) async-start(), calls=%async_computation.1 | async-start | bytes 2359296 | tf_op jit(solution)/shard_map/all_gather | solution.py:95
  7.9 148.4 %reduce-scatter.2.cloned.1.call-start = ((), (), s32[]{:S(2)}) async-start(), calls=%async_computation.2 | async-start | bytes 1179648 | tf_op jit(solution)/shard_map/reduce_scatter | solution.py:122
  11.9 7.0 %copy-start = (f32[16,4096]{1,0:T(8,128)S(1)}, f32[16,4096]{1,0:T(8,128)}, u32[]{:S(2)}) copy-start(f32[16,4096]{1,0:T(8,128)} %param.15) | copy-start | bytes 786436
  11.9 7.0 %copy-start.2 = (s32[512]{0:T(512)S(1)}, s32[512]{0:T(512)}, u32[]{:S(2)}) copy-start(s32[512]{0:T(512)} %param.11) | copy-start | bytes 6148
  65.7 21.8 %copy-start.1 = (f32[512,8]{0,1:T(8,128)S(1)}, f32[512,8]{0,1:T(8,128)}, u32[]{:S(2)}) copy-start(f32[512,8]{0,1:T(8,128)} %param.14) | copy-start | bytes 49156
  65.8 21.8 %copy-start.3 = (f32[512]{0:T(512)S(1)}, f32[512]{0:T(512)}, u32[]{:S(2)}) copy-start(f32[512]{0:T(512)} %param.13) | copy-start | bytes 6148
  121.6 76.9 %all-gather.6.cloned.1.call-start = ((), (), s32[]{:S(2)}) async-start(), calls=%async_computation.3 | async-start | bytes 1310720 | tf_op jit(solution)/shard_map/all_gather | solution.py:132
Sparse Core Ops, SparseCore 0:
  9.9 30.4 all-gather.3
  121.7 34.5 reduce-scatter.1
  170.4 27.9 all-gather.5
